TPU v7x, 256 devices: a whole 4x4x8 slice. The times are simulated.
256 devices in a mesh: ea: 64 (over y, x_lo, z), sa: 4 (over x_hi, core).
Axes of the slice: x: 4 (x_hi: 2, x_lo: 2; x = x_hi * 2 + x_lo), y: 4, z: 8, core: 2. Of those that a mesh axis runs over, the one named last changes fastest.
Arguments:
- lesser: bfloat16 [2, 1024, 2, 256, 256], P(None, 'ea', None, 'sa'), may hold values from -30 to 30, as said below
- greater: bfloat16 [2, 1024, 2, 256, 256], P(None, 'ea', None, 'sa'), may hold values from -30 to 30, as said below
Outputs:
- polar: float32 [2, 1024, 2, 256, 256], P(None, 'ea', None, 'sa')
- pol_norm: float32 [1], replicated
Inputs may be any that keep to these rules, and one draw needn't show every extreme that they name: `lesser`: Real-valued entries, independent from energy to energy. `greater`: Real-valued entries, independent from energy to energy.
All inputs are finite; a program needn't handle non-finite values.
Results may differ from a plain program's by a relative error of at most 0.0049.
Values may be sent and summed in bfloat16 or wider, within the bound.
A program may use at most 128 MiB of HBM per device.

v0:
```python
import functools
import math

import jax
import jax.numpy as jnp
from jax import lax
from jax.sharding import Mesh
from jax.sharding import PartitionSpec as P

NE = 1024
ORB = 256
BLOCKS = 2
EA = ("ea_0", "ea_1", "ea_2")
EA_SA = ("ea_0", "ea_1", "ea_2", "sa_0", "sa_1")
SA = ("sa_0", "sa_1")


def one_axis_at_a_time(shard, axes):
    return functools.reduce(lax.psum, axes, shard)


def energy_tables(count):
    index = jnp.arange(count, dtype=jnp.int32)
    phase = index[:, None] * index[None, :] % count
    angle = phase.astype(jnp.float32) * (2.0 * math.pi / count)
    return (jnp.cos(angle).astype(jnp.bfloat16), jnp.sin(angle).astype(jnp.bfloat16))


def spectra(columns, cosine, sine):
    stacked = jnp.concatenate(columns, axis=1)
    return (
        jnp.dot(cosine, stacked, preferred_element_type=jnp.float32),
        jnp.dot(sine, stacked, preferred_element_type=jnp.float32),
    )


def split_spectrum(cos_part, sin_part, which, width):
    real_cols = slice(2 * which * width, (2 * which + 1) * width)
    imag_cols = slice((2 * which + 1) * width, (2 * which + 2) * width)
    spec_re = cos_part[:, real_cols] + sin_part[:, imag_cols]
    spec_im = cos_part[:, imag_cols] - sin_part[:, real_cols]
    return (spec_re, spec_im)


def polarize(less_re, less_im, great_re, great_im, cosine, sine, count):
    width = less_re.shape[1]
    prod_re = (less_re * great_re + less_im * great_im).astype(jnp.bfloat16)
    prod_im = (less_im * great_re - less_re * great_im).astype(jnp.bfloat16)
    cos_part, sin_part = spectra([prod_re, prod_im], cosine, sine)
    corr_re = cos_part[:, :width] - sin_part[:, width:]
    corr_im = cos_part[:, width:] + sin_part[:, :width]
    weight = float(count) ** (-1.5)
    return jnp.stack([weight * corr_im, -weight * corr_re])


def both_spectra(less_pairs, great_pairs, cosine, sine):
    energies = less_pairs.shape[1]
    width = less_pairs[0].size // energies
    cos_part, sin_part = spectra(
        [
            less_pairs[0].reshape(energies, width),
            less_pairs[1].reshape(energies, width),
            great_pairs[0].reshape(energies, width),
            great_pairs[1].reshape(energies, width),
        ],
        cosine,
        sine,
    )
    less_re, less_im = split_spectrum(cos_part, sin_part, 0, width)
    great_re, great_im = split_spectrum(cos_part, sin_part, 1, width)
    return (less_re, less_im, great_re, great_im)


def body(lesser, greater):
    cosine, sine = energy_tables(NE)
    less_pairs, great_pairs = (
        lax.all_to_all(lesser, EA, split_axis=4, concat_axis=1, tiled=True),
        lax.all_to_all(greater, EA, split_axis=4, concat_axis=1, tiled=True),
    )
    shape = less_pairs.shape
    less_re, less_im, great_re, great_im = both_spectra(less_pairs, great_pairs, cosine, sine)
    polar_local = polarize(less_re, less_im, great_re, great_im, cosine, sine, NE).reshape(shape)
    total = jnp.sum(polar_local * polar_local)
    polar = lax.all_to_all(
        polar_local.astype(jnp.bfloat16), EA, split_axis=1, concat_axis=4, tiled=True
    ).astype(polar_local.dtype)
    norm_total = one_axis_at_a_time(total, EA_SA)
    pol_norm = jnp.sqrt(norm_total / (NE * BLOCKS * ORB * ORB) + 1e-06).reshape(1)
    return (polar, pol_norm)


def solution(mesh):
    finer = Mesh(mesh.devices.reshape(4, 2, 8, 2, 2), ("ea_0", "ea_1", "ea_2", "sa_0", "sa_1"))
    in_specs = (P(None, EA, None, SA, None), P(None, EA, None, SA, None))
    out_specs = (P(None, EA, None, SA, None), P())
    return jax.shard_map(body, mesh=finer, in_specs=in_specs, out_specs=out_specs, check_vma=False)
```

profile of v0, /device:TPU:4, one launch (start us, length us, event | category | flops | bytes accessed | tf_op | source)
XLA Modules:
  0.0 481.3 jit_solution(5528786645547221499)
XLA Ops:
  0.6 7.4 %copy.15 = bf16[2,16,2,64,256]{3,1,2,0,4:T(8,128)(2,1)} copy(bf16[2,16,2,64,256]{4,3,2,1,0:T(8,128)(2,1)} %param.2) | data formatting | bytes 4194304 | tf_op args[0]
  8.0 7.9 %reshape.27 = bf16[64,2,8192]{2,1,0:T(2,128)(2,1)} reshape(bf16[256,2,2,16,64]{4,3,2,1,0:T(8,128)(2,1)} %bitcast.43) | data formatting | bytes 4194304
  15.9 12.7 %all-to-all-start = ((bf16[64,2,8192]{2,1,0:T(2,128)(2,1)}), bf16[64,2,8192]{2,1,0:T(2,128)(2,1)S(1)}, u32[]{:S(2)}, u32[]{:S(2)}) async-start(bf16[64,2,8192]{2,1,0:T(2,128)(2,1)} %reshape.27), calls=%async_computation | async-start | bytes 4194304 | tf_op jit(solution)/shard_map/all_to_all | solution.py:77
  28.7 7.4 %copy.19 = bf16[2,16,2,64,256]{3,1,2,0,4:T(8,128)(2,1)} copy(bf16[2,16,2,64,256]{4,3,2,1,0:T(8,128)(2,1)} %param.3) | data formatting | bytes 4194304 | tf_op args[1]
  36.1 7.9 %reshape.29 = bf16[64,2,8192]{2,1,0:T(2,128)(2,1)} reshape(bf16[256,2,2,16,64]{4,3,2,1,0:T(8,128)(2,1)} %bitcast.44) | data formatting | bytes 4194304
  43.9 36.2 %all-to-all-done = bf16[64,2,8192]{2,1,0:T(2,128)(2,1)S(1)} async-done(((bf16[64,2,8192]{2,1,0:T(2,128)(2,1)}), bf16[64,2,8192]{2,1,0:T(2,128)(2,1)S(1)}, u32[]{:S(2)}, u32[]{:S(2)}) %all-to-all-start) | async-done | bytes 2097184 | tf_op jit(solution)/shard_map/all_to_all | solution.py:77
  80.2 6.5 %all-to-all-start.1 = ((bf16[64,2,8192]{2,1,0:T(2,128)(2,1)}), bf16[64,2,8192]{2,1,0:T(2,128)(2,1)}, u32[]{:S(2)}, u32[]{:S(2)}) async-start(bf16[64,2,8192]{2,1,0:T(2,128)(2,1)} %reshape.29), calls=%async_computation.1 | async-start | bytes 4194304 | tf_op jit(solution)/shard_map/all_to_all | solution.py:78
  86.6 4.0 reshape.28
  90.6 2.9 copy.16
  93.5 2.3 fusion.32
  95.8 41.1 %all-to-all-done.1 = bf16[64,2,8192]{2,1,0:T(2,128)(2,1)} async-done(((bf16[64,2,8192]{2,1,0:T(2,128)(2,1)}), bf16[64,2,8192]{2,1,0:T(2,128)(2,1)}, u32[]{:S(2)}, u32[]{:S(2)}) %all-to-all-start.1) | async-done | bytes 2097184 | tf_op jit(solution)/shard_map/all_to_all | solution.py:78
  136.9 7.9 %reshape.30 = bf16[256,2,2,16,64]{4,3,2,1,0:T(8,128)(2,1)} reshape(bf16[64,2,8192]{2,1,0:T(2,128)(2,1)} %all-to-all-done.1) | data formatting | bytes 4194304
  144.8 2.9 copy.20
  147.7 3.0 fusion.31
  150.7 13.6 %copy.22 = bf16[1,64,16,2,64,4]{2,1,5,4,3,0:T(8,128)(2,1)} copy(bf16[1,64,16,2,64,4]{4,2,5,1,3,0:T(8,128)(2,1)} %get-tuple-element.10) | data formatting | bytes 2097152 | tf_op jit(solution)/shard_map/slice | solution.py:64
  164.3 15.1 %reshape_squeeze.15 = bf16[1024,512]{0,1:T(8,128)(2,1)S(1)} reshape(bf16[1,64,16,2,64,4]{2,1,5,4,3,0:T(8,128)(2,1)} %copy.22) | data formatting | bytes 2097152 | tf_op jit(solution)/shard_map/reshape;squeeze | solution.py:64
  179.5 13.6 %copy.18 = bf16[1,64,16,2,64,4]{2,1,5,4,3,0:T(8,128)(2,1)} copy(bf16[1,64,16,2,64,4]{4,2,5,1,3,0:T(8,128)(2,1)} %get-tuple-element.12) | data formatting | bytes 2097152 | tf_op jit(solution)/shard_map/slice | solution.py:62
  193.1 15.8 %reshape_squeeze.13 = bf16[1024,512]{0,1:T(8,128)(2,1)} reshape(bf16[1,64,16,2,64,4]{2,1,5,4,3,0:T(8,128)(2,1)} %copy.18) | data formatting | bytes 2097152 | tf_op jit(solution)/shard_map/reshape;squeeze | solution.py:62
  208.9 25.9 %copy.21 = bf16[1,64,16,2,64,4]{2,1,5,4,3,0:T(8,128)(2,1)} copy(bf16[1,64,16,2,64,4]{4,2,5,1,3,0:T(8,128)(2,1)} %get-tuple-element.11) | data formatting | bytes 2097152 | tf_op jit(solution)/shard_map/slice | solution.py:63
  234.7 15.8 %reshape_squeeze.14 = bf16[1024,512]{0,1:T(8,128)(2,1)} reshape(bf16[1,64,16,2,64,4]{2,1,5,4,3,0:T(8,128)(2,1)} %copy.21) | data formatting | bytes 2097152 | tf_op jit(solution)/shard_map/reshape;squeeze | solution.py:63
  250.5 12.9 %copy.17 = bf16[1,64,16,2,64,4]{2,1,5,4,3,0:T(8,128)(2,1)} copy(bf16[1,64,16,2,64,4]{4,2,5,1,3,0:T(8,128)(2,1)S(1)} %get-tuple-element.13) | data formatting | bytes 2097152 | tf_op jit(solution)/shard_map/slice | solution.py:61
  263.4 15.9 %reshape_squeeze.12 = bf16[1024,512]{0,1:T(8,128)(2,1)} reshape(bf16[1,64,16,2,64,4]{2,1,5,4,3,0:T(8,128)(2,1)} %copy.17) | data formatting | bytes 2097152 | tf_op jit(solution)/shard_map/reshape;squeeze | solution.py:61
  279.3 1.4 constant_dynamic-update-slice_fusion.3
  280.7 0.1 constant_dynamic-update-slice_fusion.2
  281.0 19.4 %fusion.12 = f32[1024,2048]{1,0:T(8,128)S(1)} fusion(bf16[1024,2048]{0,1:T(8,128)(2,1)S(1)} %constant_dynamic-update-slice_fusion), kind=kOutput, calls=%fused_computation.29 | convolution fusion | flops 4310695936 | bytes 12582912 | tf_op jit(solution)/shard_map/dot_general | solution.py:33
  300.4 19.4 %fusion.10 = f32[1024,2048]{1,0:T(8,128)S(1)} fusion(bf16[1024,2048]{0,1:T(8,128)(2,1)S(1)} %constant_dynamic-update-slice_fusion), kind=kOutput, calls=%fused_computation.27 | convolution fusion | flops 4310695936 | bytes 12582912 | tf_op jit(solution)/shard_map/dot_general | solution.py:32
  319.8 2.3 add_convert_fusion
  322.1 17.0 %fusion.11 = f32[1024,1024]{0,1:T(8,128)S(1)} fusion(bf16[1024,512]{1,0:T(8,128)(2,1)S(1)} %get-tuple-element.7, bf16[1024,512]{1,0:T(8,128)(2,1)S(1)} %get-tuple-element.6), kind=kOutput, calls=%fused_computation.28 | convolution fusion | flops 2167406592 | bytes 6291456 | tf_op jit(solution)/shard_map/dot_general | solution.py:33
  339.2 17.0 %fusion.9 = f32[1024,1024]{0,1:T(8,128)S(1)} fusion(bf16[1024,512]{1,0:T(8,128)(2,1)S(1)} %get-tuple-element.7, bf16[1024,512]{1,0:T(8,128)(2,1)S(1)} %get-tuple-element.6), kind=kOutput, calls=%fused_computation.26 | convolution fusion | flops 2167406592 | bytes 6291456 | tf_op jit(solution)/shard_map/dot_general | solution.py:32
  356.1 3.0 fusion.8
  359.1 1.9 stack.9
  361.0 3.6 copy.23
  364.6 1.9 stack.10
  366.4 3.3 copy.24
  369.7 8.4 %fusion.33 = bf16[1024,2,2,4,64]{4,3,2,1,0:T(4,128)(2,1)} fusion(f32[1,1024,2,64,4]{3,4,2,0,1:T(4,128)} %copy.24, f32[1,1024,2,64,4]{3,4,2,0,1:T(4,128)} %copy.23), kind=kLoop, calls=%fused_computation.54 | loop fusion | flops 1048576 | bytes 6291456
  378.1 8.6 %reshape.31 = bf16[64,2,8192]{2,1,0:T(2,128)(2,1)} reshape(bf16[1024,2,2,4,64]{4,3,2,1,0:T(4,128)(2,1)} %fusion.33) | data formatting | bytes 4194304
  386.7 6.3 %all-to-all-start.2 = ((bf16[64,2,8192]{2,1,0:T(2,128)(2,1)}), bf16[64,2,8192]{2,1,0:T(2,128)(2,1)S(1)}, u32[]{:S(2)}, u32[]{:S(2)}) async-start(bf16[64,2,8192]{2,1,0:T(2,128)(2,1)} %reshape.31), calls=%async_computation.2 | async-start | bytes 4194304 | tf_op jit(solution)/shard_map/all_to_all | solution.py:84
  393.0 7.1 %multiply_reduce_fusion = f32[]{:T(128)} fusion(f32[1,1024,2,64,4]{3,4,2,0,1:T(4,128)} %copy.24, f32[1,1024,2,64,4]{3,4,2,0,1:T(4,128)} %copy.23), kind=kLoop, calls=%fused_computation.2 | loop fusion | flops 3145727 | bytes 4194308 | tf_op jit(solution)/shard_map/reduce_sum | solution.py:83
  400.1 11.4 %psum.35 = f32[]{:T(128)} all-reduce(f32[]{:T(128)} %multiply_reduce_fusion), channel_id=1, replica_groups=mesh['ea_0'=4,'ea_1'=2,'ea_2'=8,'sa_0'=2,'sa_1'=2] {'ea_0'}, use_global_device_ids=true, to_apply=%region_1.2 | all-reduce | flops 1 | bytes 8 | tf_op jit(solution)/shard_map/psum | solution.py:19
  411.4 5.7 %psum.36 = f32[]{:T(128)} all-reduce(f32[]{:T(128)} %psum.35), channel_id=1, replica_groups=mesh['ea_0'=4,'ea_1'=2,'ea_2'=8,'sa_0'=2,'sa_1'=2] {'ea_1'}, use_global_device_ids=true, to_apply=%region_2.3 | all-reduce | flops 1 | bytes 8 | tf_op jit(solution)/shard_map/psum | solution.py:19
  417.1 32.6 %psum.37 = f32[]{:T(128)} all-reduce(f32[]{:T(128)} %psum.36), channel_id=1, replica_groups=mesh['ea_0'=4,'ea_1'=2,'ea_2'=8,'sa_0'=2,'sa_1'=2] {'ea_2'}, use_global_device_ids=true, to_apply=%region_3.4 | all-reduce | flops 1 | bytes 8 | tf_op jit(solution)/shard_map/psum | solution.py:19
  449.7 7.1 %psum.38 = f32[]{:T(128)} all-reduce(f32[]{:T(128)} %psum.37), channel_id=1, replica_groups=mesh['ea_0'=4,'ea_1'=2,'ea_2'=8,'sa_0'=2,'sa_1'=2] {'sa_0'}, use_global_device_ids=true, to_apply=%region_4.5 | all-reduce | flops 1 | bytes 8 | tf_op jit(solution)/shard_map/psum | solution.py:19
  456.7 3.1 psum.39
  460.5 4.0 reshape.32
  464.5 3.3 copy.25
  467.8 0.9 convert_bitcast_fusion
  468.7 4.3 copy.26
  473.0 6.8 %copy.27 = f32[2,16,2,64,256]{4,3,2,1,0:T(8,128)} copy(f32[2,16,2,64,256]{3,1,4,2,0:T(8,128)} %bitcast.41) | data formatting | bytes 8388608
  (7 shorter events, 0.2 us)
Async XLA Ops:
  15.9 64.2 %all-to-all-start = ((bf16[64,2,8192]{2,1,0:T(2,128)(2,1)}), bf16[64,2,8192]{2,1,0:T(2,128)(2,1)S(1)}, u32[]{:S(2)}, u32[]{:S(2)}) async-start(bf16[64,2,8192]{2,1,0:T(2,128)(2,1)} %reshape.27), calls=%async_computation | async-start | bytes 4194304 | tf_op jit(solution)/shard_map/all_to_all | solution.py:77
  80.2 56.7 %all-to-all-start.1 = ((bf16[64,2,8192]{2,1,0:T(2,128)(2,1)}), bf16[64,2,8192]{2,1,0:T(2,128)(2,1)}, u32[]{:S(2)}, u32[]{:S(2)}) async-start(bf16[64,2,8192]{2,1,0:T(2,128)(2,1)} %reshape.29), calls=%async_computation.1 | async-start | bytes 4194304 | tf_op jit(solution)/shard_map/all_to_all | solution.py:78
  263.4 17.3 %copy-start = (bf16[1024,512]{0,1:T(8,128)(2,1)S(1)}, bf16[1024,512]{0,1:T(8,128)(2,1)}, u32[]{:S(2)}) copy-start(bf16[1024,512]{0,1:T(8,128)(2,1)} %reshape_squeeze.13) | copy-start | bytes 3145732
  279.3 1.5 copy-start.1
  386.7 73.8 %all-to-all-start.2 = ((bf16[64,2,8192]{2,1,0:T(2,128)(2,1)}), bf16[64,2,8192]{2,1,0:T(2,128)(2,1)S(1)}, u32[]{:S(2)}, u32[]{:S(2)}) async-start(bf16[64,2,8192]{2,1,0:T(2,128)(2,1)} %reshape.31), calls=%async_computation.2 | async-start | bytes 4194304 | tf_op jit(solution)/shard_map/all_to_all | solution.py:84
where the time goes:
time: 490 us; the launch traced here: 481 us
  local copies, waits for them, and re-layouts  221 us (45%)
  waiting for transfers between devices  77.3 us (16%)
  matrix products  72.8 us (15%)
  blocking collectives  59.8 us (12%)
  starting transfers between devices  25.5 us (5%)
  other arithmetic  21.7 us (4%)
    unnamed x16, local copies, waits for them, and re-layouts  63.4 us
    psum x5, blocking collectives, one_axis_at_a_time(): return functools.reduce(lax.psum, axes, shard)  59.8 us
    all_to_all x1, waiting for transfers between devices, body(): lax.all_to_all(greater, EA, split_axis=4, concat_axis=1, tiled=True)  41.1 us
    dot_general x2, matrix products, spectra(): jnp.dot(cosine, stacked, preferred_element_type=jnp.float32)  36.4 us
    dot_general x2, matrix products, spectra(): jnp.dot(sine, stacked, preferred_element_type=jnp.float32)  36.4 us
    all_to_all x1, waiting for transfers between devices, body(): lax.all_to_all(lesser, EA, split_axis=4, concat_axis=1, tiled=True)  36.2 us
    slice x1, local copies, waits for them, and re-layouts, both_spectra(): great_pairs[0].reshape(energies, width)  25.9 us
    slice x2, local copies, waits for them, and re-layouts, both_spectra(): great_pairs[1].reshape(energies, width)  16.6 us
  transfers between devices with their start and end apart: 3, of which 2 were waited for; matrix products, arithmetic and copies ran while one was open for 7% of the time, Pallas kernels for 0%

commit v1 on v0

v1 whole, which is shorter than its diff:
```python
import functools
import math

import jax
import jax.numpy as jnp
from jax import lax
from jax.experimental import pallas as pl
from jax.experimental.pallas import tpu as pltpu
from jax.sharding import Mesh
from jax.sharding import PartitionSpec as P

EA = ("ea_0", "ea_1", "ea_2")
SA = ("sa_0", "sa_1")
MESH = pl.DeviceIdType.MESH
STEP = 32
F32 = jnp.float32
BF16 = jnp.bfloat16


def base_tables(count):
    energy = jnp.arange(count, dtype=jnp.int32)
    coarse = jnp.arange(count // STEP, dtype=jnp.int32) * STEP
    fine = jnp.arange(STEP, dtype=jnp.int32)
    unit = 2.0 * math.pi / count
    tables = []
    for index in (coarse, fine):
        angle = (index[:, None] * energy[None, :] % count).astype(F32) * unit
        tables += [jnp.cos(angle), jnp.sin(angle)]
    return tables


def kernel(sizes, less_ref, great_ref, cos_hi, sin_hi, cos_lo, sin_lo, out_ref, norm_ref,
           stage, shuffle, send_in, recv_in, table_a, table_b, prod, send_out, recv_out,
           square, norm_own, norm_sa, norm_ea, norm_all,
           load_sem, send_sem, recv_in_sem, recv_out_sem, norm_sem):
    ny, nx, nz, n0, n1 = sizes
    peers = ny * nx * nz
    own, blocks, count = 16, 2, 16 * peers
    columns = less_ref.shape[-1]
    y, x, z = (lax.axis_index(a) for a in EA)
    s0, s1 = (lax.axis_index(a) for a in SA)
    me = (y * nx + x) * nz + z
    me_sa = s0 * n1 + s1

    def partner(t):
        m, q = lax.rem(t, nz), t // nz
        dz = lax.rem(m, 2) * ((m + 1) // 2) + (1 - lax.rem(m, 2)) * lax.rem(nz - m // 2, nz)
        py, px, pz = lax.rem(y + q // nx, ny), lax.rem(x + lax.rem(q, nx), nx), lax.rem(z + dz, nz)
        return (py * nx + px) * nz + pz, (py, px, pz, s0, s1)

    def partner_sa(t):
        other = lax.rem(me_sa + t, n0 * n1)
        return (y, x, z, other // n1, lax.rem(other, n1))

    loads = [pltpu.make_async_copy(ref, stage.at[n], load_sem.at[n])
             for n, ref in enumerate((less_ref, great_ref))]
    for load in loads:
        load.start()

    barrier = pltpu.get_barrier_semaphore()

    @pl.loop(1, peers)
    def _(t):
        pl.semaphore_signal(barrier, inc=1, device_id=partner(t)[1], device_id_type=MESH)

    for t in range(1, n0 * n1):
        pl.semaphore_signal(barrier, inc=1, device_id=partner_sa(t), device_id_type=MESH)

    for load in loads:
        load.wait()
    tiles = peers // 16
    for which in range(2):
        for part in range(2):

            @pl.loop(0, blocks * tiles)
            def _(n, which=which, part=part):
                block, tile = n // tiles, lax.rem(n, tiles)
                rows = pl.ds(pl.multiple_of(tile * 16, 16), 16)
                for h in range(columns // 128):
                    lanes = slice(h * 128, (h + 1) * 128)
                    shuffle[h] = stage[which, part, :, block, rows, lanes].astype(F32).reshape(own * 16, 128)
                    for i in range(16):
                        send_in[block, tile * 16 + i, 2 * which + part, :, lanes] = shuffle[
                            h, pl.ds(i, own, stride=16), :].astype(BF16)

    for block in range(blocks):
        for q in range(4):
            recv_in[block, q, me] = send_in[block, me, q]

    pl.semaphore_wait(barrier, peers - 1 + n0 * n1 - 1)

    def copy_in(block, t):
        other, device = partner(t)
        return pltpu.make_async_remote_copy(
            src_ref=send_in.at[block, other], dst_ref=recv_in.at[block, :, me],
            send_sem=send_sem.at[block], recv_sem=recv_in_sem.at[block],
            device_id=device, device_id_type=MESH)

    def copy_out(block, t):
        other, device = partner(t)
        return pltpu.make_async_remote_copy(
            src_ref=send_out.at[block, other], dst_ref=recv_out.at[block, me],
            send_sem=send_sem.at[blocks + block], recv_sem=recv_out_sem.at[block],
            device_id=device, device_id_type=MESH)

    def copy_norm(t):
        return pltpu.make_async_remote_copy(
            src_ref=norm_all, dst_ref=norm_ea.at[me],
            send_sem=norm_sem.at[2], recv_sem=norm_sem.at[3],
            device_id=partner(t)[1], device_id_type=MESH)

    def copy_norm_sa(t):
        return pltpu.make_async_remote_copy(
            src_ref=norm_own, dst_ref=norm_sa.at[me_sa],
            send_sem=norm_sem.at[0], recv_sem=norm_sem.at[1],
            device_id=partner_sa(t), device_id_type=MESH)

    def all_of(ref, sem):
        return pltpu.make_async_remote_copy(
            src_ref=ref, dst_ref=ref, send_sem=sem, recv_sem=sem,
            device_id=partner(1)[1], device_id_type=MESH)

    for block in range(blocks):

        @pl.loop(1, peers)
        def _(t, block=block):
            copy_in(block, t).start()

    @pl.loop(0, count // STEP)
    def _(n):
        c_hi, s_hi = cos_hi[pl.ds(n, 1), :], sin_hi[pl.ds(n, 1), :]
        c_lo, s_lo = cos_lo[...], sin_lo[...]
        cosine = (c_hi * c_lo - s_hi * s_lo).astype(BF16)
        sine = (s_hi * c_lo + c_hi * s_lo).astype(BF16)
        rows = pl.ds(pl.multiple_of(n * STEP, STEP), STEP)
        table_a[rows, :count] = cosine
        table_a[rows, count:] = sine
        table_b[rows, :count] = -sine
        table_b[rows, count:] = cosine

    square[...] = jnp.zeros_like(square)
    strip = min(256, count)
    weight = float(count) ** (-1.5)

    def dot(a, b):
        return jnp.dot(a, b, preferred_element_type=F32)

    for block in range(blocks):
        all_of(recv_in.at[block, :, pl.ds(0, peers - 1)], recv_in_sem.at[block]).wait_recv()

        @pl.loop(0, count // strip)
        def _(n, block=block):
            rows = pl.ds(pl.multiple_of(n * strip, strip), strip)
            rows_im = pl.ds(pl.multiple_of(n * strip + count, strip), strip)
            less = recv_in[block, 0:2].reshape(2 * count, columns)
            great = recv_in[block, 2:4].reshape(2 * count, columns)
            less_re, less_im = dot(table_a[rows, :], less), dot(table_b[rows, :], less)
            great_re, great_im = dot(table_a[rows, :], great), dot(table_b[rows, :], great)
            prod[rows, :] = (less_im * great_re - less_re * great_im).astype(BF16)
            prod[rows_im, :] = (less_re * great_re + less_im * great_im).astype(BF16)

        @pl.loop(0, count // strip)
        def _(n, block=block):
            rows = pl.ds(pl.multiple_of(n * strip, strip), strip)
            polar_re = weight * dot(table_a[rows, :], prod[...])
            polar_im = -weight * dot(table_b[rows, :], prod[...])
            for part, value in enumerate((polar_re, polar_im)):
                square[...] += jnp.sum((value * value).reshape(strip // 8, 8, columns), axis=0)
                send_out[block, pl.ds(n * (strip // own), strip // own), part] = value.astype(BF16).reshape(
                    strip // own, own, columns)

        if block == blocks - 1:
            total = jnp.sum(square[...], axis=0, keepdims=True)
            norm_own[...] = functools.reduce(
                jnp.add, [total[:, n * 128:(n + 1) * 128] for n in range(columns // 128)])
            norm_sa[me_sa] = norm_own[...]
            for t in range(1, n0 * n1):
                copy_norm_sa(t).start()
            if n0 * n1 > 1:
                all_of(norm_sa.at[pl.ds(0, n0 * n1 - 1)], norm_sem.at[1]).wait_recv()
            norm_all[...] = functools.reduce(jnp.add, [norm_sa[n] for n in range(n0 * n1)])
            norm_ea[me] = norm_all[...]

            @pl.loop(1, peers)
            def _(t):
                copy_norm(t).start()

        recv_out[block, me] = send_out[block, me]

        @pl.loop(1, peers)
        def _(t, block=block):
            copy_out(block, t).start()

    for block in range(blocks):
        all_of(recv_out.at[block, pl.ds(0, peers - 1)], recv_out_sem.at[block]).wait_recv()
        for part in range(2):

            @pl.loop(0, tiles)
            def _(tile, block=block, part=part):
                rows = pl.ds(pl.multiple_of(tile * 16, 16), 16)
                for h in range(columns // 128):
                    lanes = slice(h * 128, (h + 1) * 128)
                    for i in range(16):
                        shuffle[h, pl.ds(i, own, stride=16), :] = recv_out[
                            block, tile * 16 + i, part, :, lanes].astype(F32)
                    out_ref[part, :, block, rows, lanes] = shuffle[h].reshape(own, 16, 128).astype(out_ref.dtype)

    all_of(norm_ea.at[pl.ds(0, peers - 1)], norm_sem.at[3]).wait_recv()
    norm = jnp.sum(jnp.sum(norm_ea[...], axis=0), axis=-1, keepdims=True)
    entries = count * blocks * peers * n0 * n1 * columns
    norm_ref[...] = jnp.broadcast_to(jnp.sqrt(norm / entries + 1e-06), norm_ref.shape)

    for block in range(blocks):
        all_of(recv_in.at[block, :, pl.ds(0, peers - 1)], send_sem.at[block]).wait_send()
        all_of(recv_out.at[block, pl.ds(0, peers - 1)], send_sem.at[blocks + block]).wait_send()
    if n0 * n1 > 1:
        all_of(norm_sa.at[pl.ds(0, n0 * n1 - 1)], norm_sem.at[0]).wait_send()
    all_of(norm_ea.at[pl.ds(0, peers - 1)], norm_sem.at[2]).wait_send()


def body(sizes, lesser, greater):
    ny, nx, nz, n0, n1 = sizes
    peers = ny * nx * nz
    own, blocks = 16, 2
    count = own * peers
    columns = lesser.shape[-1]
    vmem = pl.BlockSpec(memory_space=pltpu.VMEM)
    hbm = pl.BlockSpec(memory_space=pl.ANY)
    polar, norm = pl.pallas_call(
        functools.partial(kernel, sizes),
        out_shape=[jax.ShapeDtypeStruct(lesser.shape, BF16), jax.ShapeDtypeStruct((1, 128), F32)],
        in_specs=[hbm, hbm] + [vmem] * 4,
        out_specs=[vmem, vmem],
        scratch_shapes=[
            pltpu.VMEM((2,) + lesser.shape, BF16),
            pltpu.VMEM((columns // 128, own * 16, 128), F32),
            pltpu.VMEM((blocks, peers, 4, own, columns), BF16),
            pltpu.VMEM((blocks, 4, peers, own, columns), BF16),
            pltpu.VMEM((count, 2 * count), BF16),
            pltpu.VMEM((count, 2 * count), BF16),
            pltpu.VMEM((2 * count, columns), BF16),
            pltpu.VMEM((blocks, peers, 2, own, columns), BF16),
            pltpu.VMEM((blocks, peers, 2, own, columns), BF16),
            pltpu.VMEM((8, columns), F32),
            pltpu.VMEM((1, 128), F32),
            pltpu.VMEM((n0 * n1, 1, 128), F32),
            pltpu.VMEM((peers, 1, 128), F32),
            pltpu.VMEM((1, 128), F32),
            pltpu.SemaphoreType.DMA((2,)),
            pltpu.SemaphoreType.DMA((2 * blocks,)),
            pltpu.SemaphoreType.DMA((blocks,)),
            pltpu.SemaphoreType.DMA((blocks,)),
            pltpu.SemaphoreType.DMA((4,)),
        ],
        compiler_params=pltpu.CompilerParams(
            collective_id=0, has_side_effects=True, vmem_limit_bytes=60 * 1024 * 1024),
        name="polarize",
    )(lesser, greater, *base_tables(count))
    return polar.astype(F32), norm[0, :1]


def solution(mesh):
    sizes = (4, 2, 8, 2, 2)
    finer = Mesh(mesh.devices.reshape(sizes), EA + SA)
    spec = P(None, EA, None, SA, None)
    return jax.shard_map(functools.partial(body, sizes), mesh=finer, in_specs=(spec, spec),
                         out_specs=(spec, P()), check_vma=False)
```

time: 490 us -> 163 us (0.33); the launches traced: 481 us -> 162 us
  local copies, waits for them, and re-layouts: 221 us -> 0.01 us
  Pallas kernels: 0 us -> 153 us
  waiting for transfers between devices: 77.3 us -> 0 us
  matrix products: 72.8 us -> 0 us
  blocking collectives: 59.8 us -> 0 us
  starting transfers between devices: 25.5 us -> 0 us
  other arithmetic: 21.7 us -> 6.68 us
    pallas_call x0 -> x1, Pallas kernels: none -> 153 us  [body(): pl.pallas_call(functools.partial(kernel, sizes), out_shape=[jax.ShapeDtyp...]
    all_to_all x3 -> x0, waiting for transfers between devices: 77.3 us -> none  [the longest x1 41.1 us: body(): lax.all_to_all(greater, EA, split_axis=4, concat_axis=1, tiled=True)]
    another operation x8 -> x0, local copies, waits for them, and re-layouts: 73.2 us -> none  [the longest x1 15.9 us: both_spectra(): less_pairs[0].reshape(energies, width)]
    dot_general x4 -> x0, matrix products: 72.8 us -> none  [the longest x2 36.4 us: spectra(): jnp.dot(cosine, stacked, preferred_element_type=jnp.float32)]
    slice x6 -> x0, local copies, waits for them, and re-layouts: 71.2 us -> none  [the longest x1 25.9 us: both_spectra(): great_pairs[0].reshape(energies, width)]
    unnamed x16 -> x2, local copies, waits for them, and re-layouts: 63.4 us -> 0.01 us
    psum x5 -> x0, blocking collectives: 59.8 us -> none  [one_axis_at_a_time(): return functools.reduce(lax.psum, axes, shard)]
    all_to_all x3 -> x0, starting transfers between devices: 25.5 us -> none  [the longest x1 12.7 us: body(): lax.all_to_all(lesser, EA, split_axis=4, concat_axis=1, tiled=True)]
  transfers between devices with their start and end apart: 3 -> 0, of which waited for: 2 -> 0; matrix products, arithmetic and copies ran while one was open for 7% -> 0% of each run, Pallas kernels for 0% -> 0%
where the time goes in v1:
time: 163 us; the launch traced here: 162 us
  Pallas kernels  153 us (94%)
  other arithmetic  6.68 us (4%)
  between operations  1.82 us (1%)
    pallas_call x1, Pallas kernels, body(): pl.pallas_call(functools.partial(kernel, sizes), out_shape=[jax.ShapeDtyp...  153 us
    convert_element_type x1, other arithmetic, body(): return (polar.astype(F32), norm[0, :1])  4.16 us

profile of v1, /device:TPU:4, one launch (start us, length us, event | category | flops | bytes accessed | tf_op | source)
XLA Modules:
  0.0 161.8 jit_solution(6662266283999733709)
XLA Ops:
  0.6 1.3 fusion.14
  1.9 1.2 fusion.12
  3.2 153.3 %polarize.1 = (bf16[2,16,2,64,256]{4,3,2,1,0:T(8,128)(2,1)}, f32[1,128]{1,0:T(1,128)}) custom-call(bf16[2,16,2,64,256]{4,3,2,1,0:T(8,128)(2,1)} %less_ref.1, bf16[2,16,2,64,256]{4,3,2,1,0:T(8,128)(2,1)} %great_ref.1, f32[32,1024]{1,0:T(8,128)} %get-tuple-element.7.cos_hi, f32[32,1024]{1,0:T(8,128)} %get-tuple-element.6.sin_hi, ...), custom_call_target="tpu_custom_call" | custom-call | tf_op jit(solution)/shard_map/polarize/pallas_call | solution.py:229
  156.4 0.0 copy-start
  156.5 4.2 %convert_element_type.15 = f32[2,16,2,64,256]{4,3,2,1,0:T(8,128)} convert(bf16[2,16,2,64,256]{4,3,2,1,0:T(8,128)(2,1)} %get-tuple-element.4) | non-fusion elementwise | flops 1048576 | bytes 6291456 | tf_op jit(solution)/shard_map/convert_element_type | solution.py:259
  160.6 0.0 copy-done
  (1 shorter events, 0.0 us)
Async XLA Ops:
  156.4 4.2 %copy-start = (f32[1,128]{1,0:T(1,128)S(1)}, f32[1,128]{1,0:T(1,128)}, u32[]{:S(2)}) copy-start(f32[1,128]{1,0:T(1,128)} %get-tuple-element.5) | copy-start | bytes 1540

commit v2 on v1

--- a/solution.py
+++ b/solution.py
@@ -17,20 +17,8 @@
 BF16 = jnp.bfloat16
 
 
-def base_tables(count):
-    energy = jnp.arange(count, dtype=jnp.int32)
-    coarse = jnp.arange(count // STEP, dtype=jnp.int32) * STEP
-    fine = jnp.arange(STEP, dtype=jnp.int32)
-    unit = 2.0 * math.pi / count
-    tables = []
-    for index in (coarse, fine):
-        angle = (index[:, None] * energy[None, :] % count).astype(F32) * unit
-        tables += [jnp.cos(angle), jnp.sin(angle)]
-    return tables
-
-
-def kernel(sizes, less_ref, great_ref, cos_hi, sin_hi, cos_lo, sin_lo, out_ref, norm_ref,
-           stage, shuffle, send_in, recv_in, table_a, table_b, prod, send_out, recv_out,
+def kernel(sizes, less_ref, great_ref, recv_out, norm_ref,
+           stage, shuffle, send_in, recv_in, base, table_a, table_b, prod, send_out,
            square, norm_own, norm_sa, norm_ea, norm_all,
            load_sem, send_sem, recv_in_sem, recv_out_sem, norm_sem):
     ny, nx, nz, n0, n1 = sizes
@@ -42,29 +30,34 @@
     me = (y * nx + x) * nz + z
     me_sa = s0 * n1 + s1
 
-    def partner(t):
-        m, q = lax.rem(t, nz), t // nz
-        dz = lax.rem(m, 2) * ((m + 1) // 2) + (1 - lax.rem(m, 2)) * lax.rem(nz - m // 2, nz)
-        py, px, pz = lax.rem(y + q // nx, ny), lax.rem(x + lax.rem(q, nx), nx), lax.rem(z + dz, nz)
-        return (py * nx + px) * nz + pz, (py, px, pz, s0, s1)
+    along_z = [(dz + 1) // 2 if dz % 2 else (nz - dz // 2) % nz for dz in range(nz)]
+    pz = [lax.rem(z + dz, nz) for dz in along_z]
+
+    def each_partner(visit):
+        for dz in range(1, nz):
+            visit((y * nx + x) * nz + pz[dz], (y, x, pz[dz], s0, s1))
+
+        @pl.loop(1, ny * nx)
+        def _(q):
+            py, px = lax.rem(y + q // nx, ny), lax.rem(x + lax.rem(q, nx), nx)
+            for dz in range(nz):
+                visit((py * nx + px) * nz + pz[dz], (py, px, pz[dz], s0, s1))
 
     def partner_sa(t):
         other = lax.rem(me_sa + t, n0 * n1)
         return (y, x, z, other // n1, lax.rem(other, n1))
 
-    loads = [pltpu.make_async_copy(ref, stage.at[n], load_sem.at[n])
-             for n, ref in enumerate((less_ref, great_ref))]
+    loads = [pltpu.make_async_copy(ref, to, load_sem.at[n]) for n, (ref, to) in enumerate(
+        ((less_ref, stage.at[0]), (great_ref, stage.at[1])))]
+    barrier = pltpu.get_barrier_semaphore()
+    each_partner(lambda other, device: pl.semaphore_signal(
+        barrier, inc=1, device_id=device, device_id_type=MESH))
+
+    for t in range(1, n0 * n1):
+        pl.semaphore_signal(barrier, inc=1, device_id=partner_sa(t), device_id_type=MESH)
+
     for load in loads:
         load.start()
-
-    barrier = pltpu.get_barrier_semaphore()
-
-    @pl.loop(1, peers)
-    def _(t):
-        pl.semaphore_signal(barrier, inc=1, device_id=partner(t)[1], device_id_type=MESH)
-
-    for t in range(1, n0 * n1):
-        pl.semaphore_signal(barrier, inc=1, device_id=partner_sa(t), device_id_type=MESH)
 
     for load in loads:
         load.wait()
@@ -89,25 +82,23 @@
 
     pl.semaphore_wait(barrier, peers - 1 + n0 * n1 - 1)
 
-    def copy_in(block, t):
-        other, device = partner(t)
+    def copy_in(block, other, device):
         return pltpu.make_async_remote_copy(
             src_ref=send_in.at[block, other], dst_ref=recv_in.at[block, :, me],
             send_sem=send_sem.at[block], recv_sem=recv_in_sem.at[block],
             device_id=device, device_id_type=MESH)
 
-    def copy_out(block, t):
-        other, device = partner(t)
+    def copy_out(block, other, device):
         return pltpu.make_async_remote_copy(
             src_ref=send_out.at[block, other], dst_ref=recv_out.at[block, me],
             send_sem=send_sem.at[blocks + block], recv_sem=recv_out_sem.at[block],
             device_id=device, device_id_type=MESH)
 
-    def copy_norm(t):
+    def copy_norm(other, device):
         return pltpu.make_async_remote_copy(
             src_ref=norm_all, dst_ref=norm_ea.at[me],
             send_sem=norm_sem.at[2], recv_sem=norm_sem.at[3],
-            device_id=partner(t)[1], device_id_type=MESH)
+            device_id=device, device_id_type=MESH)
 
     def copy_norm_sa(t):
         return pltpu.make_async_remote_copy(
@@ -118,18 +109,22 @@
     def all_of(ref, sem):
         return pltpu.make_async_remote_copy(
             src_ref=ref, dst_ref=ref, send_sem=sem, recv_sem=sem,
-            device_id=partner(1)[1], device_id_type=MESH)
-
-    for block in range(blocks):
-
-        @pl.loop(1, peers)
-        def _(t, block=block):
-            copy_in(block, t).start()
+            device_id=(y, x, pz[1], s0, s1), device_id_type=MESH)
+
+    for block in range(blocks):
+        each_partner(lambda other, device, block=block: copy_in(block, other, device).start())
+
+    for n, (rows, step) in enumerate(((count // STEP, STEP), (STEP, 1))):
+        row = lax.broadcasted_iota(jnp.int32, (rows, count), 0) * step
+        phase = jnp.bitwise_and(row * lax.broadcasted_iota(jnp.int32, (rows, count), 1), count - 1)
+        angle = phase.astype(F32) * (2.0 * math.pi / count)
+        base[2 * n, :rows] = jnp.cos(angle)
+        base[2 * n + 1, :rows] = jnp.sin(angle)
 
     @pl.loop(0, count // STEP)
     def _(n):
-        c_hi, s_hi = cos_hi[pl.ds(n, 1), :], sin_hi[pl.ds(n, 1), :]
-        c_lo, s_lo = cos_lo[...], sin_lo[...]
+        c_hi, s_hi = base[0, pl.ds(n, 1), :], base[1, pl.ds(n, 1), :]
+        c_lo, s_lo = base[2], base[3]
         cosine = (c_hi * c_lo - s_hi * s_lo).astype(BF16)
         sine = (s_hi * c_lo + c_hi * s_lo).astype(BF16)
         rows = pl.ds(pl.multiple_of(n * STEP, STEP), STEP)
@@ -180,30 +175,13 @@
                 all_of(norm_sa.at[pl.ds(0, n0 * n1 - 1)], norm_sem.at[1]).wait_recv()
             norm_all[...] = functools.reduce(jnp.add, [norm_sa[n] for n in range(n0 * n1)])
             norm_ea[me] = norm_all[...]
-
-            @pl.loop(1, peers)
-            def _(t):
-                copy_norm(t).start()
+            each_partner(lambda other, device: copy_norm(other, device).start())
 
         recv_out[block, me] = send_out[block, me]
-
-        @pl.loop(1, peers)
-        def _(t, block=block):
-            copy_out(block, t).start()
+        each_partner(lambda other, device, block=block: copy_out(block, other, device).start())
 
     for block in range(blocks):
         all_of(recv_out.at[block, pl.ds(0, peers - 1)], recv_out_sem.at[block]).wait_recv()
-        for part in range(2):
-
-            @pl.loop(0, tiles)
-            def _(tile, block=block, part=part):
-                rows = pl.ds(pl.multiple_of(tile * 16, 16), 16)
-                for h in range(columns // 128):
-                    lanes = slice(h * 128, (h + 1) * 128)
-                    for i in range(16):
-                        shuffle[h, pl.ds(i, own, stride=16), :] = recv_out[
-                            block, tile * 16 + i, part, :, lanes].astype(F32)
-                    out_ref[part, :, block, rows, lanes] = shuffle[h].reshape(own, 16, 128).astype(out_ref.dtype)
 
     all_of(norm_ea.at[pl.ds(0, peers - 1)], norm_sem.at[3]).wait_recv()
     norm = jnp.sum(jnp.sum(norm_ea[...], axis=0), axis=-1, keepdims=True)
@@ -216,6 +194,29 @@
     if n0 * n1 > 1:
         all_of(norm_sa.at[pl.ds(0, n0 * n1 - 1)], norm_sem.at[0]).wait_send()
     all_of(norm_ea.at[pl.ds(0, peers - 1)], norm_sem.at[2]).wait_send()
+
+
+def finish_kernel(recv_ref, out_ref, shuffle, sem):
+    blocks, rows, parts, own, columns = recv_ref.shape
+    tiles, halves = rows // 8, columns // 128
+
+    for block in range(blocks):
+        for part in range(parts):
+
+            @pl.loop(0, tiles)
+            def _(tile, block=block, part=part):
+                slot = (block * parts + part) * tiles + tile
+                for i in range(8):
+                    value = recv_ref[block, tile * 8 + i, part].astype(F32)
+                    for h in range(halves):
+                        shuffle[slot, h, pl.ds(i, own, stride=8), :] = value[:, h * 128:(h + 1) * 128]
+                for h in range(halves):
+                    pltpu.make_async_copy(
+                        shuffle.at[slot, h].reshape(own, 8, 128),
+                        out_ref.at[part, :, block, pl.ds(pl.multiple_of(tile * 8, 8), 8), h * 128:(h + 1) * 128],
+                        sem).start()
+
+    pltpu.make_async_copy(out_ref, out_ref, sem).wait()
 
 
 def body(sizes, lesser, greater):
@@ -225,22 +226,23 @@
     count = own * peers
     columns = lesser.shape[-1]
     vmem = pl.BlockSpec(memory_space=pltpu.VMEM)
-    hbm = pl.BlockSpec(memory_space=pl.ANY)
-    polar, norm = pl.pallas_call(
+    hbm = pl.BlockSpec(memory_space=pltpu.HBM)
+    received = (blocks, peers, 2, own, columns)
+    raw, norm = pl.pallas_call(
         functools.partial(kernel, sizes),
-        out_shape=[jax.ShapeDtypeStruct(lesser.shape, BF16), jax.ShapeDtypeStruct((1, 128), F32)],
-        in_specs=[hbm, hbm] + [vmem] * 4,
+        out_shape=[jax.ShapeDtypeStruct(received, BF16), jax.ShapeDtypeStruct((1, 128), F32)],
+        in_specs=[hbm] * 2,
         out_specs=[vmem, vmem],
         scratch_shapes=[
             pltpu.VMEM((2,) + lesser.shape, BF16),
             pltpu.VMEM((columns // 128, own * 16, 128), F32),
             pltpu.VMEM((blocks, peers, 4, own, columns), BF16),
             pltpu.VMEM((blocks, 4, peers, own, columns), BF16),
+            pltpu.VMEM((4, STEP, count), F32),
             pltpu.VMEM((count, 2 * count), BF16),
             pltpu.VMEM((count, 2 * count), BF16),
             pltpu.VMEM((2 * count, columns), BF16),
-            pltpu.VMEM((blocks, peers, 2, own, columns), BF16),
-            pltpu.VMEM((blocks, peers, 2, own, columns), BF16),
+            pltpu.VMEM(received, BF16),
             pltpu.VMEM((8, columns), F32),
             pltpu.VMEM((1, 128), F32),
             pltpu.VMEM((n0 * n1, 1, 128), F32),
@@ -253,10 +255,22 @@
             pltpu.SemaphoreType.DMA((4,)),
         ],
         compiler_params=pltpu.CompilerParams(
-            collective_id=0, has_side_effects=True, vmem_limit_bytes=60 * 1024 * 1024),
+            collective_id=0, has_side_effects=True, vmem_limit_bytes=51 * 1024 * 1024),
         name="polarize",
-    )(lesser, greater, *base_tables(count))
-    return polar.astype(F32), norm[0, :1]
+    )(lesser, greater)
+    polar = pl.pallas_call(
+        finish_kernel,
+        out_shape=jax.ShapeDtypeStruct(lesser.shape, F32),
+        in_specs=[vmem],
+        out_specs=hbm,
+        scratch_shapes=[
+            pltpu.VMEM((2 * blocks * (peers // 8), columns // 128, own * 8, 128), F32),
+            pltpu.SemaphoreType.DMA,
+        ],
+        compiler_params=pltpu.CompilerParams(vmem_limit_bytes=16 * 1024 * 1024),
+        name="finish",
+    )(raw)
+    return polar, norm[0, :1]
 
 
 def solution(mesh):

time: 163 us -> 156 us (0.957)
  other arithmetic: 6.68 us -> 0 us
    convert_element_type x1 -> x0, other arithmetic: 4.16 us -> none  [body(): return (polar.astype(F32), norm[0, :1])]
    sin x2 -> x0, other arithmetic: 2.51 us -> none  [base_tables(): tables += [jnp.cos(angle), jnp.sin(angle)]]
    pallas_call x0 -> x1, Pallas kernels: none -> 1.99 us  [body(): pl.pallas_call(finish_kernel, out_shape=jax.ShapeDtypeStruct(lesser.shape...]
    pallas_call x1, Pallas kernels: 153 us -> 152 us  [body(): pl.pallas_call(functools.partial(kernel, sizes), out_shape=[jax.ShapeDtyp...]
where the time goes in v2:
time: 156 us; the launch traced here: 155 us
  Pallas kernels  154 us (99%)
  between operations  1.8 us (1%)
    pallas_call x1, Pallas kernels, body(): pl.pallas_call(functools.partial(kernel, sizes), out_shape=[jax.ShapeDtyp...  152 us

profile of v2, /device:TPU:4, one launch (start us, length us, event | category | flops | bytes accessed | tf_op | source)
XLA Modules:
  0.0 155.4 jit_solution(5863978242284288738)
XLA Ops:
  0.6 151.6 %polarize.1 = (bf16[2,64,2,16,256]{4,3,2,1,0:T(8,128)(2,1)S(1)}, f32[1,128]{1,0:T(1,128)S(1)}) custom-call(bf16[2,16,2,64,256]{4,3,2,1,0:T(8,128)(2,1)} %less_ref.1, bf16[2,16,2,64,256]{4,3,2,1,0:T(8,128)(2,1)} %great_ref.1), custom_call_target="tpu_custom_call" | custom-call | tf_op jit(solution)/shard_map/polarize/pallas_call | solution.py:231
  152.2 2.0 %finish.1 = f32[2,16,2,64,256]{4,3,2,1,0:T(8,128)} custom-call(bf16[2,64,2,16,256]{4,3,2,1,0:T(8,128)(2,1)S(1)} %get-tuple-element.4.recv_ref), custom_call_target="tpu_custom_call" | custom-call | tf_op jit(solution)/shard_map/finish/pallas_call | solution.py:261
